TPU v7x, 32 devices: a whole 2x2x4 slice. The times are simulated.
32 devices in a mesh: gx: 4 (over y, core), gy: 8 (over z, x).
Axes of the slice: x: 2, y: 2, z: 4, core: 2. Of those that a mesh axis runs over, the one named last changes fastest.
Arguments:
- pixels: int32 [16, 16, 4, 131072], P('gy', 'gx'), may hold values from 0 to 255, as said below
- weights: bfloat16 [16, 16, 4, 131072], P('gy', 'gx'), may hold values from 0.25 to 1
- adjacency: int32 [2, 16, 16], replicated, may hold values 0 or 1
Outputs:
- log_gain: float32 [16, 16], P('gy', 'gx')
Inputs may be any that keep to these rules, and one draw needn't show every extreme that they name: `pixels`: bin indices of 8-bit intensities. `adjacency`: entry [0, r, c] is 1 where tile (r, c) and the tile to its right share a usable border, entry [1, r, c] likewise for the tile below; entries of pairs beyond the grid's edge are read by no output.
All inputs are finite; a program needn't handle non-finite values.
Results may differ from a plain program's by a relative error of at most 0.0003.
Values may be sent and summed in bfloat16 or wider, within the bound.
A program may use at most 128 MiB of HBM per device.

v0:
```python
import functools
import jax
import jax.numpy as jnp
from jax import lax
from jax.experimental import pallas as pl
from jax.experimental.pallas import tpu as pltpu
from jax.sharding import PartitionSpec as P

ITERS = 20
WIDTH = 4096
SUBS = 4
PER_DOT = 4


anchor_weight = 0.5
mismatch_scale = 8.0


def chunk_width(length):
    width = WIDTH
    while length % width:
        width //= 2
    return width


def one_hots(bins, joint, level, shape):
    bins16 = jnp.broadcast_to(bins, shape).astype(jnp.int16)
    upper = (bins16 & 240) == level * 16
    lower = (bins16 & 15) == level
    joint16 = jnp.broadcast_to(joint, shape).astype(jnp.bfloat16)
    zero = jnp.zeros(shape, jnp.bfloat16)
    return jnp.where(upper, joint16, zero), jnp.where(lower, jnp.ones(shape, jnp.bfloat16), zero)


def accumulate(dots, read_bins, read_joint, sums, width):
    depth = width // SUBS
    shape = (16, depth)
    level = lax.broadcasted_iota(jnp.int32, shape, 0).astype(jnp.int16)
    for index, strips in enumerate(dots):
        left, right = [], []
        for strip in strips:
            for sub in range(SUBS):
                lanes = slice(sub * depth, (sub + 1) * depth)
                first, second = one_hots(read_bins(strip, lanes), read_joint(strip, lanes), level, shape)
                left.append(first)
                right.append(second)
        left = jnp.concatenate(left, axis=0)
        right = jnp.concatenate(right, axis=0)
        counts = lax.dot_general(
            left, right, (((1,), (1,)), ((), ())), preferred_element_type=jnp.float32
        )
        sums[index] += counts


def finish(dots, sums, out_ref):
    place = 0
    for index, strips in enumerate(dots):
        for number in range(len(strips)):
            total = jnp.zeros((16, 16), jnp.float32)
            for sub in range(SUBS):
                start = (number * SUBS + sub) * 16
                total += sums[index, start : start + 16, start : start + 16]
            out_ref[place] = total
            place += 1


def group(strips):
    return [strips[i : i + PER_DOT] for i in range(0, len(strips), PER_DOT)]


def inner_strips(rows, columns):
    strips = []
    for row in range(rows - 1):
        for column in range(columns):
            strips += [(row, column, 1), (row + 1, column, 0)]
    for row in range(rows):
        for column in range(columns - 1):
            strips += [(row, column, 3), (row, column + 1, 2)]
    return strips


def outer_strips(rows, columns):
    strips = [(0, column, 0) for column in range(columns)]
    strips += [(rows - 1, column, 1) for column in range(columns)]
    strips += [(row, 0, 2) for row in range(rows)]
    strips += [(row, columns - 1, 3) for row in range(rows)]
    return strips


def partner_of(strip):
    row, column, side = strip
    return [
        (row - 1, column, 1),
        (row + 1, column, 0),
        (row, column - 1, 3),
        (row, column + 1, 2),
    ][side]


def edges_kernel(w_ref, up_ref, down_ref, left_ref, right_ref):
    rows, columns = w_ref.shape[:2]
    for column in range(columns):
        up_ref[column : column + 1] = w_ref[0, column, 0:1, :]
        down_ref[column : column + 1] = w_ref[rows - 1, column, 1:2, :]
    for row in range(rows):
        left_ref[row : row + 1] = w_ref[row, 0, 2:3, :]
        right_ref[row : row + 1] = w_ref[row, columns - 1, 3:4, :]


def edges(weights):
    rows, columns, sides, length = weights.shape
    width = chunk_width(length)
    row_shape = jax.ShapeDtypeStruct((columns, length), weights.dtype)
    column_shape = jax.ShapeDtypeStruct((rows, length), weights.dtype)
    row_spec = pl.BlockSpec((columns, width), lambda i: (0, i))
    column_spec = pl.BlockSpec((rows, width), lambda i: (0, i))
    return pl.pallas_call(
        edges_kernel,
        grid=(length // width,),
        in_specs=[pl.BlockSpec((rows, columns, sides, width), lambda i: (0, 0, 0, i))],
        out_specs=[row_spec, row_spec, column_spec, column_spec],
        out_shape=[row_shape, row_shape, column_shape, column_shape],
        name="edges",
    )(weights)


def inner_kernel(dots, p_ref, w_ref, out_ref, wide, sums):
    @pl.when(pl.program_id(0) == 0)
    def _():
        sums[...] = jnp.zeros_like(sums)

    wide[...] = w_ref[...].astype(jnp.float32)

    def read_bins(strip, lanes):
        row, column, side = strip
        return p_ref[row, column, side : side + 1, lanes]

    def read_joint(strip, lanes):
        row, column, side = strip
        if side in (0, 2):
            row, column, side = partner_of(strip)
        other_row, other_column, other_side = partner_of((row, column, side))
        return (
            wide[row, column, side : side + 1, lanes]
            * wide[other_row, other_column, other_side : other_side + 1, lanes]
        )

    accumulate(dots, read_bins, read_joint, sums, p_ref.shape[-1])

    @pl.when(pl.program_id(0) == pl.num_programs(0) - 1)
    def _():
        finish(dots, sums, out_ref)


def outer_kernel(dots, p_ref, w_ref, up_ref, down_ref, left_ref, right_ref, out_ref, wide, row_wide, column_wide, sums):
    @pl.when(pl.program_id(0) == 0)
    def _():
        sums[...] = jnp.zeros_like(sums)

    wide[...] = w_ref[...].astype(jnp.float32)
    row_wide[0] = up_ref[...].astype(jnp.float32)
    row_wide[1] = down_ref[...].astype(jnp.float32)
    column_wide[0] = left_ref[...].astype(jnp.float32)
    column_wide[1] = right_ref[...].astype(jnp.float32)

    def read_bins(strip, lanes):
        row, column, side = strip
        return p_ref[row, column, side : side + 1, lanes]

    def read_joint(strip, lanes):
        row, column, side = strip
        own = wide[row, column, side : side + 1, lanes]
        if side < 2:
            return own * row_wide[side, column : column + 1, lanes]
        return own * column_wide[side - 2, row : row + 1, lanes]

    accumulate(dots, read_bins, read_joint, sums, p_ref.shape[-1])

    @pl.when(pl.program_id(0) == pl.num_programs(0) - 1)
    def _():
        finish(dots, sums, out_ref)


def strip_sums(kernel, strips, pixels, weights, halos, name):
    rows, columns, sides, length = pixels.shape
    width = chunk_width(length)
    dots = group(strips)
    block = (rows, columns, sides, width)
    halo_specs = [pl.BlockSpec((h.shape[0], width), lambda i: (0, i)) for h in halos]
    scratch = [pltpu.VMEM(block, jnp.float32)]
    if halos:
        scratch += [pltpu.VMEM((2, columns, width), jnp.float32), pltpu.VMEM((2, rows, width), jnp.float32)]
    scratch += [pltpu.VMEM((len(dots), 16 * SUBS * PER_DOT, 16 * SUBS * PER_DOT), jnp.float32)]
    return pl.pallas_call(
        functools.partial(kernel, dots),
        grid=(length // width,),
        in_specs=[pl.BlockSpec(block, lambda i: (0, 0, 0, i))] * 2 + halo_specs,
        out_specs=pl.BlockSpec((len(strips), 16, 16), lambda i: (0, 0, 0)),
        out_shape=jax.ShapeDtypeStruct((len(strips), 16, 16), jnp.float32),
        scratch_shapes=scratch,
        compiler_params=pltpu.CompilerParams(vmem_limit_bytes=56 * 1024 * 1024),
        cost_estimate=pl.CostEstimate(
            flops=len(strips) * length * 256 * 32,
            bytes_accessed=rows * columns * sides * length * 6,
            transcendentals=0,
        ),
        name=name,
    )(pixels, weights, *halos)


def shift(array, axis, step):
    count = lax.axis_size(axis)
    if step > 0:
        pairs = [(i, i + 1) for i in range(count - 1)]
    else:
        pairs = [(i + 1, i) for i in range(count - 1)]
    return lax.ppermute(array, axis, pairs)


def histograms(pixels, weights):
    rows, columns, sides, length = pixels.shape
    up, down, left, right = edges(weights)
    from_up = shift(down, "gy", 1)
    from_down = shift(up, "gy", -1)
    from_left = shift(right, "gx", 1)
    from_right = shift(left, "gx", -1)
    inner = inner_strips(rows, columns)
    outer = outer_strips(rows, columns)
    inner_sums = strip_sums(inner_kernel, inner, pixels, weights, [], "inner")
    outer_sums = strip_sums(
        outer_kernel, outer, pixels, weights, [from_up, from_down, from_left, from_right], "outer"
    )
    sums = jnp.concatenate([inner_sums, outer_sums], axis=0).reshape(-1, 256)
    place = {strip: i for i, strip in enumerate(inner + outer)}
    order = [place[(r, c, s)] for r in range(rows) for c in range(columns) for s in range(sides)]
    return jnp.stack([sums[i] for i in order]).reshape(rows, columns, sides, 256)


def padded_2(block, sides, width):
    for axis, dim in sides:
        count = lax.axis_size(axis)
        forward = [(i, i + 1) for i in range(count - 1)]
        backward = [(target, source) for source, target in forward]
        low = lax.ppermute(
            lax.slice_in_dim(block, block.shape[dim] - width, None, axis=dim), axis, forward
        )
        high = lax.ppermute(lax.slice_in_dim(block, 0, width, axis=dim), axis, backward)
        block = jnp.concatenate([low, block, high], axis=dim)
    return block


def column_edges(source):
    return jnp.stack([source[:, 0, 2], source[:, -1, 3]], axis=1)


def row_edges(source):
    return jnp.stack([source[0, :, 0], source[-1, :, 1]], axis=0)


def facing(source, column_halo, row_halo):
    side_right = jnp.concatenate([source[:, 1:, 2], column_halo[:, 3:4]], axis=1)
    side_left = jnp.concatenate([column_halo[:, 0:1], source[:, :-1, 3]], axis=1)
    side_down = jnp.concatenate([source[1:, :, 0], row_halo[3:4]], axis=0)
    side_up = jnp.concatenate([row_halo[0:1], source[:-1, :, 1]], axis=0)
    return jnp.stack([side_up, side_down, side_left, side_right], axis=2)


def strip_stats(strip_hist):
    indices = jnp.arange(256, dtype=jnp.int32)
    triangle = (indices[:, None] <= indices[None, :]).astype(jnp.float32)
    totals = jnp.sum(strip_hist, axis=-1)
    centres = indices.astype(jnp.float32) + 0.5
    means = jnp.sum(strip_hist * centres, axis=-1) / totals
    cumulative = jnp.dot(strip_hist, triangle, precision=lax.Precision.HIGHEST) / totals[..., None]
    return (means, cumulative)


def pair_terms(own_hist, other_hist, usable):
    own_mean, own_cdf = strip_stats(own_hist)
    other_mean, other_cdf = strip_stats(other_hist)
    distance = jnp.sum(jnp.abs(own_cdf - other_cdf), axis=-1)
    mismatch = (distance - jnp.abs(own_mean - other_mean)) / mismatch_scale
    present = usable > 0
    confidence = jnp.where(present, 1.0 / (0.25 + mismatch * mismatch), 0.0)
    offsets = jnp.where(present, jnp.log(other_mean) - jnp.log(own_mean), 0.0)
    return (confidence, offsets)


def relax_step(padded, confidence, offsets):
    beside = jnp.stack(
        [padded[:-2, 1:-1], padded[2:, 1:-1], padded[1:-1, :-2], padded[1:-1, 2:]], axis=-1
    )
    return jnp.sum(confidence * (beside + offsets), axis=-1)


def body(pixels, weights, adjacency):
    tile_rows, tile_columns = (pixels.shape[0], pixels.shape[1])
    grid_rows = tile_rows * lax.axis_size("gy")
    grid_columns = tile_columns * lax.axis_size("gx")
    row_start = lax.axis_index("gy") * tile_rows
    column_start = lax.axis_index("gx") * tile_columns
    tile_count = grid_rows * grid_columns
    strip_hist = histograms(pixels, weights)
    column_hist = padded_2(column_edges(strip_hist), (("gx", 1),), 1)
    row_hist = padded_2(row_edges(strip_hist), (("gy", 0),), 1)
    partner_hist = facing(strip_hist, column_hist, row_hist)
    padded_links = jnp.pad(adjacency, ((0, 0), (1, 1), (1, 1)))
    block_shape = (tile_rows, tile_columns)
    global_row = row_start + jnp.arange(tile_rows, dtype=jnp.int32)[:, None]
    global_column = column_start + jnp.arange(tile_columns, dtype=jnp.int32)[None, :]
    up_valid = lax.dynamic_slice(padded_links[1], (row_start, column_start + 1), block_shape)
    down_valid = lax.dynamic_slice(padded_links[1], (row_start + 1, column_start + 1), block_shape)
    down_valid = down_valid * (global_row < grid_rows - 1).astype(jnp.int32)
    left_valid = lax.dynamic_slice(padded_links[0], (row_start + 1, column_start), block_shape)
    right_valid = lax.dynamic_slice(padded_links[0], (row_start + 1, column_start + 1), block_shape)
    right_valid = right_valid * (global_column < grid_columns - 1).astype(jnp.int32)
    usable = jnp.stack([up_valid, down_valid, left_valid, right_valid], axis=-1)
    confidence, offsets = pair_terms(strip_hist, partner_hist, usable)
    pair_rows = jnp.stack(
        [confidence[..., 1], offsets[..., 1], confidence[..., 3], offsets[..., 3]], axis=0
    )
    gathered = lax.all_gather(pair_rows[None], ("gx", "gy"), axis=0, tiled=True)
    width_x = lax.axis_size("gx")
    width_y = lax.axis_size("gy")
    full_grid = gathered.reshape(width_x, width_y, 4, tile_rows, tile_columns)
    full_grid = full_grid.transpose(2, 1, 3, 0, 4).reshape(4, grid_rows, grid_columns)
    down_conf, down_offset = (full_grid[0], full_grid[1])
    right_conf, right_offset = (full_grid[2], full_grid[3])
    up_conf = jnp.pad(down_conf[:-1], ((1, 0), (0, 0)))
    up_offset = -jnp.pad(down_offset[:-1], ((1, 0), (0, 0)))
    left_conf = jnp.pad(right_conf[:, :-1], ((0, 0), (1, 0)))
    left_offset = -jnp.pad(right_offset[:, :-1], ((0, 0), (1, 0)))
    global_conf = jnp.stack([up_conf, down_conf, left_conf, right_conf], axis=-1)
    global_offset = jnp.stack([up_offset, down_offset, left_offset, right_offset], axis=-1)
    global_denominator = anchor_weight + jnp.sum(global_conf, axis=-1)

    def global_sweep(sweep_index, log_gain):
        updated = relax_step(jnp.pad(log_gain, 1), global_conf, global_offset) / global_denominator
        return updated - jnp.sum(updated) / tile_count

    whole_gain = lax.fori_loop(
        0, ITERS, global_sweep, jnp.zeros((grid_rows, grid_columns), jnp.float32)
    )
    return lax.dynamic_slice(whole_gain, (row_start, column_start), block_shape)


def solution(mesh):
    return jax.shard_map(
        body,
        mesh=mesh,
        in_specs=(P("gy", "gx", None, None), P("gy", "gx", None, None), P()),
        out_specs=P("gy", "gx"),
        check_vma=False,
    )
```

profile of v0, /device:TPU:0, one launch (start us, length us, event | category | flops | bytes accessed | tf_op | source)
XLA Modules:
  0.0 218.1 jit_solution(8497369943367579949)
XLA Ops:
  0.0 18.6 %edges.1 = (bf16[4,131072]{1,0:T(4,128)(2,1)}, bf16[4,131072]{1,0:T(4,128)(2,1)}, bf16[2,131072]{1,0:T(2,128)(2,1)}, bf16[2,131072]{1,0:T(2,128)(2,1)}) custom-call(bf16[2,4,4,131072]{3,2,1,0:T(4,128)(2,1)} %w_ref.5), custom_call_target="tpu_custom_call" | custom-call | tf_op jit(solution)/shard_map/edges/pallas_call | solution.py:117
  18.6 4.9 %collective-permute-start = (bf16[4,131072]{1,0:T(4,128)(2,1)}, bf16[4,131072]{1,0:T(4,128)(2,1)S(1)}, u32[]{:S(2)}, u32[]{:S(2)}) collective-permute-start(bf16[4,131072]{1,0:T(4,128)(2,1)} %get-tuple-element.74), channel_id=1, source_target_pairs={{0,1},{1,2},{2,3},{3,4},{4,5},{5,6},{6,7},{8,9},{9,10},{10,11},{11... | collective-permute-start | bytes 3145736 | tf_op jit(solution)/shard_map/ppermute | solution.py:217
  23.5 1.3 collective-permute-start.1
  24.8 1.5 collective-permute-start.2
  26.4 1.3 collective-permute-start.3
  27.7 34.8 %inner.1 = f32[20,16,16]{2,1,0:T(8,128)} custom-call(s32[2,4,4,131072]{3,2,1,0:T(4,128)} %p_ref.3, bf16[2,4,4,131072]{3,2,1,0:T(4,128)(2,1)} %w_ref.5), custom_call_target="tpu_custom_call" | custom-call | flops 21474836480 | bytes 25165824 | tf_op jit(solution)/shard_map/inner/pallas_call | solution.py:194
  62.5 0.9 fusion.16
  63.4 0.7 slice.411
  65.8 0.1 dynamic-slice_bitcast_fusion.1
  65.9 0.1 copy.47
  66.0 0.1 copy.46
  66.1 0.1 copy.48
  66.2 0.1 copy.49
  66.4 2.3 %collective-permute-done.up_ref = bf16[4,131072]{1,0:T(4,128)(2,1)S(1)} collective-permute-done((bf16[4,131072]{1,0:T(4,128)(2,1)}, bf16[4,131072]{1,0:T(4,128)(2,1)S(1)}, u32[]{:S(2)}, u32[]{:S(2)}) %collective-permute-start) | collective-permute-done | bytes 1048608 | tf_op jit(solution)/shard_map/ppermute | solution.py:217
  68.7 1.0 copy-done.1
  69.7 1.0 copy-done.2
  70.6 31.4 %outer.1 = f32[12,16,16]{2,1,0:T(8,128)} custom-call(s32[2,4,4,131072]{3,2,1,0:T(4,128)} %p_ref.3, bf16[2,4,4,131072]{3,2,1,0:T(4,128)(2,1)} %w_ref.5, bf16[4,131072]{1,0:T(4,128)(2,1)} %copy-done.1, bf16[4,131072]{1,0:T(4,128)(2,1)} %copy-done.2, bf16[2,131072]{1,0:T(2,128)(2,1)} %copy-done.3, bf16[2,131072]{1,0:T(2,128)(2,1)} %copy-done.4), custom_call_target="tpu_custom_call" | custom-call | flops 12884901888 | bytes 25165824 | tf_op jit(solution)/shard_map/outer/pallas_call | solution.py:194
  102.0 0.9 fusion.18
  103.9 0.1 stack.83
  104.1 0.1 fusion.13
  104.2 0.1 div.46
  104.3 0.2 convolution_divide_fusion.1
  104.5 0.1 copy.60
  104.6 4.3 %collective-permute-start.4 = (f32[1,4,256]{2,0,1:T(1,128)S(1)}, f32[1,4,256]{2,0,1:T(1,128)S(1)}, u32[]{:S(2)}, u32[]{:S(2)}) collective-permute-start(f32[1,4,256]{2,0,1:T(1,128)S(1)} %get-tuple-element.155), channel_id=1, source_target_pairs={{0,1},{1,2},{2,3},{3,4},{4,5},{5,6},{6,7},{8,9},{9,10},{10,11},{11... | collective-permute-start | bytes 12296 | tf_op jit(solution)/shard_map/ppermute | solution.py:244
  108.9 1.3 collective-permute-start.5
  110.2 2.6 %collective-permute-start.6 = (f32[2,1,256]{2,1,0:T(1,128)S(1)}, f32[2,1,256]{2,1,0:T(1,128)S(1)}, u32[]{:S(2)}, u32[]{:S(2)}) collective-permute-start(f32[2,1,256]{2,1,0:T(1,128)S(1)} %get-tuple-element.159), channel_id=1, source_target_pairs={{0,8},{8,16},{16,24},{1,9},{9,17},{17,25},{2,10},{10,18},{18,26},{... | collective-permute-start | bytes 6152 | tf_op jit(solution)/shard_map/ppermute | solution.py:244
  112.8 1.3 collective-permute-start.7
  114.1 0.1 reduce_sum.88
  114.2 0.1 copy.59
  114.3 3.0 %collective-permute-done.7 = f32[2,1,256]{2,1,0:T(1,128)S(1)} collective-permute-done((f32[2,1,256]{2,1,0:T(1,128)S(1)}, f32[2,1,256]{2,1,0:T(1,128)S(1)}, u32[]{:S(2)}, u32[]{:S(2)}) %collective-permute-start.7) | collective-permute-done | bytes 2080 | tf_op jit(solution)/shard_map/ppermute | solution.py:247
  117.4 0.1 fusion.14
  117.6 0.1 copy.58
  117.7 0.3 fusion.8
  118.0 0.1 copy.61
  118.1 0.1 copy.62
  118.2 0.1 copy.63
  118.3 0.1 copy.64
  118.4 0.1 copy.65
  118.5 69.3 %all-gather = f32[128,2,4]{2,1,0:T(2,128)S(1)} all-gather(f32[4,2,4]{2,1,0:T(2,128)S(1)} %pad_maximum_fusion.3), channel_id=2, replica_groups=mesh['gx'=4,'gy'=8] {'gx','gy'}, dimensions={0}, use_global_device_ids=true | all-gather | bytes 4224 | tf_op jit(solution)/shard_map/all_gather | solution.py:322
  187.8 0.1 copy.76
  187.9 0.1 squeeze.34
  188.5 0.1 stack_squeeze.45
  188.8 28.6 %while.13 = (s32[]{:T(128)}, f32[16,16]{1,0:T(8,128)S(1)}, f32[16,16,4]{1,0,2:T(8,128)S(1)}, f32[16,16,4]{1,0,2:T(8,128)S(1)}, f32[16,16]{1,0:T(8,128)S(1)}, /*index=5*/s32[]{:T(128)}, s32[]{:T(128)}, f32[]{:T(128)}) while((s32[]{:T(128)}, f32[16,16]{1,0:T(8,128)S(1)}, f32[16,16,4]{1,0,2:T(8,128)S(1)}, f32[16,16,4]{1,0,2:T(8,128)S(1)}, ...), condition=%wide.region_8.9_spmd.clone, body=%wide.region_5.8_spmd.clone.sunk | while | flops 6915 | bytes 25715 | solution.py:341
  188.9 0.7 fusion.28
  190.3 0.7 fusion.28
  191.8 0.7 fusion.28
  193.2 0.7 fusion.28
  194.6 0.7 fusion.28
  196.1 0.7 fusion.28
  197.5 0.7 fusion.28
  198.9 0.7 fusion.28
  200.4 0.7 fusion.28
  201.8 0.7 fusion.28
  203.2 0.7 fusion.28
  204.7 0.7 fusion.28
  206.1 0.7 fusion.28
  207.5 0.7 fusion.28
  209.0 0.7 fusion.28
  210.4 0.7 fusion.28
  211.8 0.7 fusion.28
  213.3 0.7 fusion.28
  214.7 0.7 fusion.28
  216.1 0.7 fusion.28
  217.4 0.6 dynamic_slice.25
  (160 shorter events, 5.6 us)
Async XLA Ops:
  18.6 50.1 %collective-permute-start = (bf16[4,131072]{1,0:T(4,128)(2,1)}, bf16[4,131072]{1,0:T(4,128)(2,1)S(1)}, u32[]{:S(2)}, u32[]{:S(2)}) collective-permute-start(bf16[4,131072]{1,0:T(4,128)(2,1)} %get-tuple-element.74), channel_id=1, source_target_pairs={{0,1},{1,2},{2,3},{3,4},{4,5},{5,6},{6,7},{8,9},{9,10},{10,11},{11... | collective-permute-start | bytes 3145736 | tf_op jit(solution)/shard_map/ppermute | solution.py:217
  23.5 45.1 %collective-permute-start.1 = (bf16[4,131072]{1,0:T(4,128)(2,1)}, bf16[4,131072]{1,0:T(4,128)(2,1)S(1)}, u32[]{:S(2)}, u32[]{:S(2)}) collective-permute-start(bf16[4,131072]{1,0:T(4,128)(2,1)} %get-tuple-element.75), channel_id=1, source_target_pairs={{1,0},{2,1},{3,2},{4,3},{5,4},{6,5},{7,6},{9,8},{10,9},{11,10},{12... | collective-permute-start | bytes 3145736 | tf_op jit(solution)/shard_map/ppermute | solution.py:217
  24.8 41.5 %collective-permute-start.2 = (bf16[2,131072]{1,0:T(2,128)(2,1)}, bf16[2,131072]{1,0:T(2,128)(2,1)S(1)}, u32[]{:S(2)}, u32[]{:S(2)}) collective-permute-start(bf16[2,131072]{1,0:T(2,128)(2,1)} %get-tuple-element.76), channel_id=1, source_target_pairs={{0,8},{8,16},{16,24},{1,9},{9,17},{17,25},{2,10},{10,18},{18,26},{... | collective-permute-start | bytes 1572872 | tf_op jit(solution)/shard_map/ppermute | solution.py:217
  26.3 39.4 %copy-start = (s32[2,16,16]{2,1,0:T(8,128)S(1)}, s32[2,16,16]{2,1,0:T(8,128)}, u32[]{:S(2)}) copy-start(s32[2,16,16]{2,1,0:T(8,128)} %param.7) | copy-start | bytes 6148
  26.4 40.0 %collective-permute-start.3 = (bf16[2,131072]{1,0:T(2,128)(2,1)}, bf16[2,131072]{1,0:T(2,128)(2,1)S(1)}, u32[]{:S(2)}, u32[]{:S(2)}) collective-permute-start(bf16[2,131072]{1,0:T(2,128)(2,1)} %get-tuple-element.77), channel_id=1, source_target_pairs={{8,0},{16,8},{24,16},{9,1},{17,9},{25,17},{10,2},{18,10},{26,18},{... | collective-permute-start | bytes 1572872 | tf_op jit(solution)/shard_map/ppermute | solution.py:217
  66.4 2.3 %copy-start.3 = (bf16[2,131072]{1,0:T(2,128)(2,1)}, bf16[2,131072]{1,0:T(2,128)(2,1)S(1)}, u32[]{:S(2)}) copy-start(bf16[2,131072]{1,0:T(2,128)(2,1)S(1)} %collective-permute-done.2.left_ref) | copy-start | bytes 1572868
  66.4 2.3 %copy-start.4 = (bf16[2,131072]{1,0:T(2,128)(2,1)}, bf16[2,131072]{1,0:T(2,128)(2,1)S(1)}, u32[]{:S(2)}) copy-start(bf16[2,131072]{1,0:T(2,128)(2,1)S(1)} %collective-permute-done.3.right_ref) | copy-start | bytes 1572868
  68.7 1.0 copy-start.1
  69.7 1.0 copy-start.2
  104.6 12.8 %collective-permute-start.4 = (f32[1,4,256]{2,0,1:T(1,128)S(1)}, f32[1,4,256]{2,0,1:T(1,128)S(1)}, u32[]{:S(2)}, u32[]{:S(2)}) collective-permute-start(f32[1,4,256]{2,0,1:T(1,128)S(1)} %get-tuple-element.155), channel_id=1, source_target_pairs={{0,1},{1,2},{2,3},{3,4},{4,5},{5,6},{6,7},{8,9},{9,10},{10,11},{11... | collective-permute-start | bytes 12296 | tf_op jit(solution)/shard_map/ppermute | solution.py:244
  108.9 8.6 %collective-permute-start.5 = (f32[1,4,256]{2,0,1:T(1,128)S(1)}, f32[1,4,256]{2,0,1:T(1,128)S(1)}, u32[]{:S(2)}, u32[]{:S(2)}) collective-permute-start(f32[1,4,256]{2,0,1:T(1,128)S(1)} %get-tuple-element.157), channel_id=1, source_target_pairs={{1,0},{2,1},{3,2},{4,3},{5,4},{6,5},{7,6},{9,8},{10,9},{11,10},{12... | collective-permute-start | bytes 12296 | tf_op jit(solution)/shard_map/ppermute | solution.py:247
  110.2 4.2 %collective-permute-start.6 = (f32[2,1,256]{2,1,0:T(1,128)S(1)}, f32[2,1,256]{2,1,0:T(1,128)S(1)}, u32[]{:S(2)}, u32[]{:S(2)}) collective-permute-start(f32[2,1,256]{2,1,0:T(1,128)S(1)} %get-tuple-element.159), channel_id=1, source_target_pairs={{0,8},{8,16},{16,24},{1,9},{9,17},{17,25},{2,10},{10,18},{18,26},{... | collective-permute-start | bytes 6152 | tf_op jit(solution)/shard_map/ppermute | solution.py:244
  112.8 4.6 %collective-permute-start.7 = (f32[2,1,256]{2,1,0:T(1,128)S(1)}, f32[2,1,256]{2,1,0:T(1,128)S(1)}, u32[]{:S(2)}, u32[]{:S(2)}) collective-permute-start(f32[2,1,256]{2,1,0:T(1,128)S(1)} %get-tuple-element.160), channel_id=1, source_target_pairs={{8,0},{16,8},{24,16},{9,1},{17,9},{25,17},{10,2},{18,10},{26,18},{... | collective-permute-start | bytes 6152 | tf_op jit(solution)/shard_map/ppermute | solution.py:247
where the time goes:
time: 221 us; the launch traced here: 218 us
  Pallas kernels  84.9 us (38%)
  blocking collectives  69.3 us (31%)
  starting transfers between devices  18.5 us (8%)
  other arithmetic  14.5 us (7%)
  loops' own time  13.2 us (6%)
  local copies, waits for them, and re-layouts  11.6 us (5%)
  waiting for transfers between devices  5.32 us (2%)
    all_gather x1, blocking collectives, body(): gathered = lax.all_gather(pair_rows[None], ('gx', 'gy'), axis=0, tiled=True)  69.3 us
    pallas_call x2, Pallas kernels, strip_sums(): pl.pallas_call(functools.partial(kernel, dots), grid=(length // width,),...  66.3 us
    pallas_call x1, Pallas kernels, edges(): pl.pallas_call(edges_kernel, grid=(length // width,), in_specs=[pl.BlockS...  18.6 us
    reduce_sum x20, other arithmetic, global_sweep(): return updated - jnp.sum(updated) / tile_count  13.4 us
    another operation x1, loops' own time, body(): lax.fori_loop(0, ITERS, global_sweep, jnp.zeros((grid_rows, grid_columns)...  13.2 us
    ppermute x4, starting transfers between devices, shift(): return lax.ppermute(array, axis, pairs)  9 us
    ppermute x2, starting transfers between devices, padded_2(): lax.ppermute(lax.slice_in_dim(block, block.shape[dim] - width, None, axis...  6.89 us
    slice x35, local copies, waits for them, and re-layouts, histograms(): sums[i]  5.03 us
  transfers between devices with their start and end apart: 8, of which 2 were waited for; matrix products, arithmetic and copies ran while one was open for 2% of the time, Pallas kernels for 16%

commit v1 on v0

--- a/solution.py
+++ b/solution.py
@@ -217,8 +217,230 @@
     return lax.ppermute(array, axis, pairs)
 
 
-def histograms(pixels, weights):
-    rows, columns, sides, length = pixels.shape
+def settle_kernel(
+    inner, outer, shape, inner_ref, outer_ref, adjacency_ref, out_ref,
+    row_in, column_in, own, other, tile, board, grid,
+    near_send, near_recv, far_send, far_recv,
+):
+    rows, columns = shape
+    x_count, y_count = lax.axis_size("gx"), lax.axis_size("gy")
+    x_index, y_index = lax.axis_index("gx"), lax.axis_index("gy")
+    devices = x_count * y_count
+    me = x_index * y_count + y_index
+    grid_rows, grid_columns = y_count * rows, x_count * columns
+    lanes = grid.shape[1]
+
+    def device(index):
+        return {"gx": index // y_count, "gy": index % y_count}
+
+    barrier = pltpu.get_barrier_semaphore()
+
+    @pl.loop(1, devices)
+    def _(step):
+        pl.semaphore_signal(
+            barrier, inc=1, device_id=device((me + step) % devices), device_id_type=pl.DeviceIdType.MESH
+        )
+
+    pl.semaphore_wait(barrier, devices - 1)
+
+    up_copy = pltpu.make_async_remote_copy(
+        src_ref=outer_ref.at[pl.ds(0, columns)], dst_ref=row_in,
+        send_sem=near_send.at[0], recv_sem=near_recv.at[0],
+        device_id={"gx": x_index, "gy": (y_index + y_count - 1) % y_count},
+        device_id_type=pl.DeviceIdType.MESH,
+    )
+    left_copy = pltpu.make_async_remote_copy(
+        src_ref=outer_ref.at[pl.ds(2 * columns, rows)], dst_ref=column_in,
+        send_sem=near_send.at[1], recv_sem=near_recv.at[1],
+        device_id={"gx": (x_index + x_count - 1) % x_count, "gy": y_index},
+        device_id_type=pl.DeviceIdType.MESH,
+    )
+    up_copy.start()
+    left_copy.start()
+
+    where_inner = {strip: i for i, strip in enumerate(inner)}
+    where_outer = {strip: i for i, strip in enumerate(outer)}
+
+    def local(strip):
+        if strip in where_inner:
+            return inner_ref[where_inner[strip]]
+        return outer_ref[where_outer[strip]]
+
+    pairs = [(r, c, 1) for r in range(rows) for c in range(columns)]
+    pairs += [(r, c, 3) for r in range(rows) for c in range(columns)]
+    late = []
+    for number, strip in enumerate(pairs):
+        own[number] = local(strip)
+        facing_strip = partner_of(strip)
+        if facing_strip in where_inner:
+            other[number] = local(facing_strip)
+        else:
+            late.append((number, strip))
+    up_copy.wait()
+    left_copy.wait()
+    for number, (row, column, side) in late:
+        other[number] = row_in[column] if side == 1 else column_in[row]
+
+    count = len(pairs)
+    centre = (
+        16 * lax.broadcasted_iota(jnp.int32, (count, 16, 16), 1)
+        + lax.broadcasted_iota(jnp.int32, (count, 16, 16), 2)
+    ).astype(jnp.float32) + 0.5
+
+    def over_bins(values):
+        return jnp.sum(jnp.sum(values, axis=1, keepdims=True), axis=2, keepdims=True)
+
+    def share_and_mean(values):
+        total = over_bins(values)
+        total = jnp.where(total > 0.0, total, 1.0)
+        return values / total, over_bins(values * centre) / total
+
+    own_share, own_mean = share_and_mean(own[...])
+    other_share, other_mean = share_and_mean(other[...])
+    gap = (own_share - other_share).reshape(count * 16, 16)
+    low_a = lax.broadcasted_iota(jnp.int32, (16, 16), 0)
+    low_b = lax.broadcasted_iota(jnp.int32, (16, 16), 1)
+    high_a = lax.broadcasted_iota(jnp.int32, (count * 16, count * 16), 0)
+    high_b = lax.broadcasted_iota(jnp.int32, (count * 16, count * 16), 1)
+    within = (low_a <= low_b).astype(jnp.float32)
+    before = ((high_a // 16 == high_b // 16) & (high_b < high_a)).astype(jnp.float32)
+    exact = dict(precision=lax.Precision.HIGHEST, preferred_element_type=jnp.float32)
+    running = jnp.dot(gap, within, **exact) + jnp.sum(
+        jnp.dot(before, gap, **exact), axis=1, keepdims=True
+    )
+    distance = over_bins(jnp.abs(running).reshape(count, 16, 16))
+    mismatch = (distance - jnp.abs(own_mean - other_mean)) / mismatch_scale
+    confidence = (1.0 / (0.25 + mismatch * mismatch)).reshape(count, 1)
+    offset = (jnp.log(other_mean) - jnp.log(own_mean)).reshape(count, 1)
+
+    pair = lax.broadcasted_iota(jnp.int32, (count, lanes), 0)
+    lane = lax.broadcasted_iota(jnp.int32, (count, lanes), 1)
+    direction = pair // (rows * columns)
+    pair_row = (pair % (rows * columns)) // columns
+    spot = 2 * direction * grid_columns + x_index * columns + pair % columns
+    placed = jnp.where(lane == spot, confidence, 0.0) + jnp.where(lane == spot + grid_columns, offset, 0.0)
+    for row in range(rows):
+        tile[row : row + 1] = jnp.sum(jnp.where(pair_row == row, placed, 0.0), axis=0, keepdims=True)
+    board[x_index, y_index] = tile[...]
+
+    def spread(index, source):
+        return pltpu.make_async_remote_copy(
+            src_ref=tile, dst_ref=board.at[source // y_count, source % y_count],
+            send_sem=far_send.at[index], recv_sem=far_recv.at[source],
+            device_id=device(index), device_id_type=pl.DeviceIdType.MESH,
+        )
+
+    @pl.loop(1, devices)
+    def _(step):
+        spread((me + step) % devices, me).start()
+
+    @pl.loop(1, devices)
+    def _(step):
+        source = (me + step) % devices
+        spread(source, source).wait_recv()
+
+    for place in range(y_count):
+        rows_here = board[0, place]
+        for other_x in range(1, x_count):
+            rows_here += board[other_x, place]
+        grid[place * rows : (place + 1) * rows] = rows_here
+
+    whole = grid[...]
+    row_id = lax.broadcasted_iota(jnp.int32, (grid_rows, lanes), 0)
+    lane_id = lax.broadcasted_iota(jnp.int32, (grid_rows, lanes), 1)
+
+    def quantity(number, link, keep):
+        values = whole if number == 0 else pltpu.roll(whole, lanes - number * grid_columns, 1)
+        return jnp.where(keep, values, 0.0)
+
+    def widened(index):
+        flat = adjacency_ref[index]
+        if lanes > grid_columns:
+            blank = jnp.zeros((grid_rows, lanes - grid_columns), jnp.int32)
+            flat = jnp.concatenate([flat, blank], axis=1)
+        return flat
+
+    keep_down = (widened(1) > 0) & (row_id < grid_rows - 1) & (lane_id < grid_columns)
+    keep_right = (widened(0) > 0) & (lane_id < grid_columns - 1)
+    down_conf = quantity(0, 1, keep_down)
+    down_off = quantity(1, 1, keep_down)
+    right_conf = quantity(2, 0, keep_right)
+    right_off = quantity(3, 0, keep_right)
+    up_conf, up_off = pltpu.roll(down_conf, 1, 0), -pltpu.roll(down_off, 1, 0)
+    left_conf, left_off = pltpu.roll(right_conf, 1, 1), -pltpu.roll(right_off, 1, 1)
+    confidence_sum = up_conf + down_conf + left_conf + right_conf
+    denominator = anchor_weight + confidence_sum
+    push = (
+        up_conf * up_off + down_conf * down_off + left_conf * left_off + right_conf * right_off
+    ) / denominator
+    up_part, down_part = up_conf / denominator, down_conf / denominator
+    left_part, right_part = left_conf / denominator, right_conf / denominator
+    pull = confidence_sum / denominator
+    tiles = grid_rows * grid_columns
+
+    def mean_of(values):
+        return jnp.sum(jnp.sum(values, axis=0, keepdims=True), axis=1, keepdims=True) / tiles
+
+    def sweep(_, fresh):
+        return (
+            up_part * pltpu.roll(fresh, 1, 0)
+            + down_part * pltpu.roll(fresh, grid_rows - 1, 0)
+            + left_part * pltpu.roll(fresh, 1, 1)
+            + right_part * pltpu.roll(fresh, lanes - 1, 1)
+            + push
+        ) - pull * mean_of(fresh)
+
+    fresh = lax.fori_loop(0, ITERS - 1, sweep, push)
+    log_gain = fresh - mean_of(fresh)
+    result = jnp.zeros((rows, columns), jnp.float32)
+    out_row = lax.broadcasted_iota(jnp.int32, (rows, columns), 0)
+    out_column = lax.broadcasted_iota(jnp.int32, (rows, columns), 1)
+    for row in range(rows):
+        line = jnp.sum(jnp.where(row_id == y_index * rows + row, log_gain, 0.0), axis=0, keepdims=True)
+        for column in range(columns):
+            value = jnp.sum(
+                jnp.where(lane_id[:1] == x_index * columns + column, line, 0.0), axis=1, keepdims=True
+            )
+            result += jnp.where((out_row == row) & (out_column == column), value, 0.0)
+    out_ref[...] = result
+
+    @pl.loop(1, devices)
+    def _(step):
+        spread((me + step) % devices, me).wait_send()
+
+
+def settle(inner, outer, shape, inner_sums, outer_sums, adjacency):
+    rows, columns = shape
+    x_count, y_count = lax.axis_size("gx"), lax.axis_size("gy")
+    devices = x_count * y_count
+    lanes = -(-4 * x_count * columns // 128) * 128
+    pairs = 2 * rows * columns
+    vmem = pl.BlockSpec(memory_space=pltpu.VMEM)
+    return pl.pallas_call(
+        functools.partial(settle_kernel, inner, outer, shape),
+        in_specs=[vmem] * 3,
+        out_specs=vmem,
+        out_shape=jax.ShapeDtypeStruct((rows, columns), jnp.float32),
+        scratch_shapes=[
+            pltpu.VMEM((columns, 16, 16), jnp.float32),
+            pltpu.VMEM((rows, 16, 16), jnp.float32),
+            pltpu.VMEM((pairs, 16, 16), jnp.float32),
+            pltpu.VMEM((pairs, 16, 16), jnp.float32),
+            pltpu.VMEM((rows, lanes), jnp.float32),
+            pltpu.VMEM((x_count, y_count, rows, lanes), jnp.float32),
+            pltpu.VMEM((y_count * rows, lanes), jnp.float32),
+            pltpu.SemaphoreType.DMA((2,)),
+            pltpu.SemaphoreType.DMA((2,)),
+            pltpu.SemaphoreType.DMA((devices,)),
+            pltpu.SemaphoreType.DMA((devices,)),
+        ],
+        compiler_params=pltpu.CompilerParams(collective_id=0, has_side_effects=True),
+        name="settle",
+    )(inner_sums, outer_sums, adjacency)
+
+
+def body(pixels, weights, adjacency):
+    rows, columns = pixels.shape[:2]
     up, down, left, right = edges(weights)
     from_up = shift(down, "gy", 1)
     from_down = shift(up, "gy", -1)
@@ -230,118 +452,7 @@
     outer_sums = strip_sums(
         outer_kernel, outer, pixels, weights, [from_up, from_down, from_left, from_right], "outer"
     )
-    sums = jnp.concatenate([inner_sums, outer_sums], axis=0).reshape(-1, 256)
-    place = {strip: i for i, strip in enumerate(inner + outer)}
-    order = [place[(r, c, s)] for r in range(rows) for c in range(columns) for s in range(sides)]
-    return jnp.stack([sums[i] for i in order]).reshape(rows, columns, sides, 256)
-
-
-def padded_2(block, sides, width):
-    for axis, dim in sides:
-        count = lax.axis_size(axis)
-        forward = [(i, i + 1) for i in range(count - 1)]
-        backward = [(target, source) for source, target in forward]
-        low = lax.ppermute(
-            lax.slice_in_dim(block, block.shape[dim] - width, None, axis=dim), axis, forward
-        )
-        high = lax.ppermute(lax.slice_in_dim(block, 0, width, axis=dim), axis, backward)
-        block = jnp.concatenate([low, block, high], axis=dim)
-    return block
-
-
-def column_edges(source):
-    return jnp.stack([source[:, 0, 2], source[:, -1, 3]], axis=1)
-
-
-def row_edges(source):
-    return jnp.stack([source[0, :, 0], source[-1, :, 1]], axis=0)
-
-
-def facing(source, column_halo, row_halo):
-    side_right = jnp.concatenate([source[:, 1:, 2], column_halo[:, 3:4]], axis=1)
-    side_left = jnp.concatenate([column_halo[:, 0:1], source[:, :-1, 3]], axis=1)
-    side_down = jnp.concatenate([source[1:, :, 0], row_halo[3:4]], axis=0)
-    side_up = jnp.concatenate([row_halo[0:1], source[:-1, :, 1]], axis=0)
-    return jnp.stack([side_up, side_down, side_left, side_right], axis=2)
-
-
-def strip_stats(strip_hist):
-    indices = jnp.arange(256, dtype=jnp.int32)
-    triangle = (indices[:, None] <= indices[None, :]).astype(jnp.float32)
-    totals = jnp.sum(strip_hist, axis=-1)
-    centres = indices.astype(jnp.float32) + 0.5
-    means = jnp.sum(strip_hist * centres, axis=-1) / totals
-    cumulative = jnp.dot(strip_hist, triangle, precision=lax.Precision.HIGHEST) / totals[..., None]
-    return (means, cumulative)
-
-
-def pair_terms(own_hist, other_hist, usable):
-    own_mean, own_cdf = strip_stats(own_hist)
-    other_mean, other_cdf = strip_stats(other_hist)
-    distance = jnp.sum(jnp.abs(own_cdf - other_cdf), axis=-1)
-    mismatch = (distance - jnp.abs(own_mean - other_mean)) / mismatch_scale
-    present = usable > 0
-    confidence = jnp.where(present, 1.0 / (0.25 + mismatch * mismatch), 0.0)
-    offsets = jnp.where(present, jnp.log(other_mean) - jnp.log(own_mean), 0.0)
-    return (confidence, offsets)
-
-
-def relax_step(padded, confidence, offsets):
-    beside = jnp.stack(
-        [padded[:-2, 1:-1], padded[2:, 1:-1], padded[1:-1, :-2], padded[1:-1, 2:]], axis=-1
-    )
-    return jnp.sum(confidence * (beside + offsets), axis=-1)
-
-
-def body(pixels, weights, adjacency):
-    tile_rows, tile_columns = (pixels.shape[0], pixels.shape[1])
-    grid_rows = tile_rows * lax.axis_size("gy")
-    grid_columns = tile_columns * lax.axis_size("gx")
-    row_start = lax.axis_index("gy") * tile_rows
-    column_start = lax.axis_index("gx") * tile_columns
-    tile_count = grid_rows * grid_columns
-    strip_hist = histograms(pixels, weights)
-    column_hist = padded_2(column_edges(strip_hist), (("gx", 1),), 1)
-    row_hist = padded_2(row_edges(strip_hist), (("gy", 0),), 1)
-    partner_hist = facing(strip_hist, column_hist, row_hist)
-    padded_links = jnp.pad(adjacency, ((0, 0), (1, 1), (1, 1)))
-    block_shape = (tile_rows, tile_columns)
-    global_row = row_start + jnp.arange(tile_rows, dtype=jnp.int32)[:, None]
-    global_column = column_start + jnp.arange(tile_columns, dtype=jnp.int32)[None, :]
-    up_valid = lax.dynamic_slice(padded_links[1], (row_start, column_start + 1), block_shape)
-    down_valid = lax.dynamic_slice(padded_links[1], (row_start + 1, column_start + 1), block_shape)
-    down_valid = down_valid * (global_row < grid_rows - 1).astype(jnp.int32)
-    left_valid = lax.dynamic_slice(padded_links[0], (row_start + 1, column_start), block_shape)
-    right_valid = lax.dynamic_slice(padded_links[0], (row_start + 1, column_start + 1), block_shape)
-    right_valid = right_valid * (global_column < grid_columns - 1).astype(jnp.int32)
-    usable = jnp.stack([up_valid, down_valid, left_valid, right_valid], axis=-1)
-    confidence, offsets = pair_terms(strip_hist, partner_hist, usable)
-    pair_rows = jnp.stack(
-        [confidence[..., 1], offsets[..., 1], confidence[..., 3], offsets[..., 3]], axis=0
-    )
-    gathered = lax.all_gather(pair_rows[None], ("gx", "gy"), axis=0, tiled=True)
-    width_x = lax.axis_size("gx")
-    width_y = lax.axis_size("gy")
-    full_grid = gathered.reshape(width_x, width_y, 4, tile_rows, tile_columns)
-    full_grid = full_grid.transpose(2, 1, 3, 0, 4).reshape(4, grid_rows, grid_columns)
-    down_conf, down_offset = (full_grid[0], full_grid[1])
-    right_conf, right_offset = (full_grid[2], full_grid[3])
-    up_conf = jnp.pad(down_conf[:-1], ((1, 0), (0, 0)))
-    up_offset = -jnp.pad(down_offset[:-1], ((1, 0), (0, 0)))
-    left_conf = jnp.pad(right_conf[:, :-1], ((0, 0), (1, 0)))
-    left_offset = -jnp.pad(right_offset[:, :-1], ((0, 0), (1, 0)))
-    global_conf = jnp.stack([up_conf, down_conf, left_conf, right_conf], axis=-1)
-    global_offset = jnp.stack([up_offset, down_offset, left_offset, right_offset], axis=-1)
-    global_denominator = anchor_weight + jnp.sum(global_conf, axis=-1)
-
-    def global_sweep(sweep_index, log_gain):
-        updated = relax_step(jnp.pad(log_gain, 1), global_conf, global_offset) / global_denominator
-        return updated - jnp.sum(updated) / tile_count
-
-    whole_gain = lax.fori_loop(
-        0, ITERS, global_sweep, jnp.zeros((grid_rows, grid_columns), jnp.float32)
-    )
-    return lax.dynamic_slice(whole_gain, (row_start, column_start), block_shape)
+    return settle(inner, outer, (rows, columns), inner_sums, outer_sums, adjacency)
 
 
 def solution(mesh):

time: 221 us -> 125 us (0.57)
  blocking collectives: 69.3 us -> 0 us
  Pallas kernels: 84.9 us -> 105 us
  other arithmetic: 14.5 us -> 0 us
  loops' own time: 13.2 us -> 0 us
  starting transfers between devices: 18.5 us -> 9 us
  local copies, waits for them, and re-layouts: 11.6 us -> 3.22 us
    all_gather x1 -> x0, blocking collectives: 69.3 us -> none  [body(): gathered = lax.all_gather(pair_rows[None], ('gx', 'gy'), axis=0, tiled=True)]
    pallas_call x0 -> x1, Pallas kernels: none -> 19.6 us  [settle(): pl.pallas_call(functools.partial(settle_kernel, inner, outer, shape), in_...]
    reduce_sum x42 -> x0, other arithmetic: 13.9 us -> none  [the longest x20 13.4 us: global_sweep(): return updated - jnp.sum(updated) / tile_count]
    another operation x1 -> x0, loops' own time: 13.2 us -> none  [body(): lax.fori_loop(0, ITERS, global_sweep, jnp.zeros((grid_rows, grid_columns)...]
    ppermute x4 -> x0, starting transfers between devices: 9.48 us -> none  [the longest x2 6.89 us: padded_2(): lax.ppermute(lax.slice_in_dim(block, block.shape[dim] - width, None, axis...]
    slice x44 -> x0, local copies, waits for them, and re-layouts: 5.51 us -> none  [the longest x35 5.03 us: histograms(): sums[i]]
    ppermute x4, waiting for transfers between devices: 2.27 us -> 6.15 us  [shift(): return lax.ppermute(array, axis, pairs)]
    ppermute x4 -> x0, waiting for transfers between devices: 3.05 us -> none  [the longest x2 3.04 us: padded_2(): lax.ppermute(lax.slice_in_dim(block, 0, width, axis=dim), axis, backward)]
  transfers between devices with their start and end apart: 8 -> 4, of which waited for: 2 -> 1; matrix products, arithmetic and copies ran while one was open for 2% -> 0% of each run, Pallas kernels for 16% -> 28%
where the time goes in v1:
time: 125 us; the launch traced here: 123 us
  Pallas kernels  105 us (84%)
  starting transfers between devices  9 us (7%)
  waiting for transfers between devices  6.15 us (5%)
  local copies, waits for them, and re-layouts  3.22 us (3%)
    pallas_call x2, Pallas kernels, strip_sums(): pl.pallas_call(functools.partial(kernel, dots), grid=(length // width,),...  66.3 us
    pallas_call x1, Pallas kernels, settle(): pl.pallas_call(functools.partial(settle_kernel, inner, outer, shape), in_...  19.6 us
    pallas_call x1, Pallas kernels, edges(): pl.pallas_call(edges_kernel, grid=(length // width,), in_specs=[pl.BlockS...  18.6 us
    ppermute x4, starting transfers between devices, shift(): return lax.ppermute(array, axis, pairs)  9 us
    ppermute x4, waiting for transfers between devices, shift(): return lax.ppermute(array, axis, pairs)  6.15 us
    unnamed x9, local copies, waits for them, and re-layouts  3.22 us
  transfers between devices with their start and end apart: 4, of which 1 were waited for; matrix products, arithmetic and copies ran while one was open for 0% of the time, Pallas kernels for 28%

profile of v1, /device:TPU:0, one launch (start us, length us, event | category | flops | bytes accessed | tf_op | source)
XLA Modules:
  0.0 122.9 jit_solution(17069438596007446779)
XLA Ops:
  0.0 18.6 %edges.1 = (bf16[4,131072]{1,0:T(4,128)(2,1)}, bf16[4,131072]{1,0:T(4,128)(2,1)}, bf16[2,131072]{1,0:T(2,128)(2,1)}, bf16[2,131072]{1,0:T(2,128)(2,1)}) custom-call(bf16[2,4,4,131072]{3,2,1,0:T(4,128)(2,1)} %w_ref.5), custom_call_target="tpu_custom_call" | custom-call | tf_op jit(solution)/shard_map/edges/pallas_call | solution.py:117
  18.6 4.9 %collective-permute-start = (bf16[4,131072]{1,0:T(4,128)(2,1)}, bf16[4,131072]{1,0:T(4,128)(2,1)S(1)}, u32[]{:S(2)}, u32[]{:S(2)}) collective-permute-start(bf16[4,131072]{1,0:T(4,128)(2,1)} %get-tuple-element.9), channel_id=1, source_target_pairs={{0,1},{1,2},{2,3},{3,4},{4,5},{5,6},{6,7},{8,9},{9,10},{10,11},{11... | collective-permute-start | bytes 3145736 | tf_op jit(solution)/shard_map/ppermute | solution.py:217
  23.5 1.3 %collective-permute-start.1 = (bf16[4,131072]{1,0:T(4,128)(2,1)}, bf16[4,131072]{1,0:T(4,128)(2,1)S(1)}, u32[]{:S(2)}, u32[]{:S(2)}) collective-permute-start(bf16[4,131072]{1,0:T(4,128)(2,1)} %get-tuple-element.10), channel_id=1, source_target_pairs={{1,0},{2,1},{3,2},{4,3},{5,4},{6,5},{7,6},{9,8},{10,9},{11,10},{12... | collective-permute-start | bytes 3145736 | tf_op jit(solution)/shard_map/ppermute | solution.py:217
  24.8 1.5 %collective-permute-start.2 = (bf16[2,131072]{1,0:T(2,128)(2,1)}, bf16[2,131072]{1,0:T(2,128)(2,1)S(1)}, u32[]{:S(2)}, u32[]{:S(2)}) collective-permute-start(bf16[2,131072]{1,0:T(2,128)(2,1)} %get-tuple-element.11), channel_id=1, source_target_pairs={{0,8},{8,16},{16,24},{1,9},{9,17},{17,25},{2,10},{10,18},{18,26},{... | collective-permute-start | bytes 1572872 | tf_op jit(solution)/shard_map/ppermute | solution.py:217
  26.3 1.3 %collective-permute-start.3 = (bf16[2,131072]{1,0:T(2,128)(2,1)}, bf16[2,131072]{1,0:T(2,128)(2,1)S(1)}, u32[]{:S(2)}, u32[]{:S(2)}) collective-permute-start(bf16[2,131072]{1,0:T(2,128)(2,1)} %get-tuple-element.12), channel_id=1, source_target_pairs={{8,0},{16,8},{24,16},{9,1},{17,9},{25,17},{10,2},{18,10},{26,18},{... | collective-permute-start | bytes 1572872 | tf_op jit(solution)/shard_map/ppermute | solution.py:217
  27.6 34.9 %inner.1.inner_ref = f32[20,16,16]{2,1,0:T(8,128)} custom-call(s32[2,4,4,131072]{3,2,1,0:T(4,128)} %p_ref.3, bf16[2,4,4,131072]{3,2,1,0:T(4,128)(2,1)} %w_ref.5), custom_call_target="tpu_custom_call" | custom-call | flops 21474836480 | bytes 25165824 | tf_op jit(solution)/shard_map/inner/pallas_call | solution.py:194
  62.5 0.0 collective-permute-done.2.left_ref
  62.5 0.0 copy-start.2
  62.5 0.0 collective-permute-done.3.right_ref
  62.5 0.0 copy-start.3
  62.5 6.1 %collective-permute-done.up_ref = bf16[4,131072]{1,0:T(4,128)(2,1)S(1)} collective-permute-done((bf16[4,131072]{1,0:T(4,128)(2,1)}, bf16[4,131072]{1,0:T(4,128)(2,1)S(1)}, u32[]{:S(2)}, u32[]{:S(2)}) %collective-permute-start) | collective-permute-done | bytes 1048608 | tf_op jit(solution)/shard_map/ppermute | solution.py:217
  68.6 0.0 copy-start
  68.6 0.0 collective-permute-done.1.down_ref
  68.7 0.0 copy-done.2
  68.7 0.0 copy-done.3
  68.7 1.0 copy-done
  69.7 0.0 copy-start.1
  69.7 1.0 copy-done.1
  70.6 31.4 %outer.1.outer_ref = f32[12,16,16]{2,1,0:T(8,128)} custom-call(s32[2,4,4,131072]{3,2,1,0:T(4,128)} %p_ref.3, bf16[2,4,4,131072]{3,2,1,0:T(4,128)(2,1)} %w_ref.5, bf16[4,131072]{1,0:T(4,128)(2,1)} %copy-done, bf16[4,131072]{1,0:T(4,128)(2,1)} %copy-done.1, bf16[2,131072]{1,0:T(2,128)(2,1)} %copy-done.2, bf16[2,131072]{1,0:T(2,128)(2,1)} %copy-done.3), custom_call_target="tpu_custom_call" | custom-call | flops 12884901888 | bytes 25165824 | tf_op jit(solution)/shard_map/outer/pallas_call | solution.py:194
  102.1 19.6 %settle.1 = f32[2,4]{1,0:T(2,128)} custom-call(f32[20,16,16]{2,1,0:T(8,128)} %inner.1.inner_ref, f32[12,16,16]{2,1,0:T(8,128)} %outer.1.outer_ref, s32[2,16,16]{2,1,0:T(8,128)} %adjacency_ref.1), custom_call_target="tpu_custom_call" | custom-call | tf_op jit(solution)/shard_map/settle/pallas_call | solution.py:419
  121.7 1.2 copy.5
Async XLA Ops:
  18.6 50.1 %collective-permute-start = (bf16[4,131072]{1,0:T(4,128)(2,1)}, bf16[4,131072]{1,0:T(4,128)(2,1)S(1)}, u32[]{:S(2)}, u32[]{:S(2)}) collective-permute-start(bf16[4,131072]{1,0:T(4,128)(2,1)} %get-tuple-element.9), channel_id=1, source_target_pairs={{0,1},{1,2},{2,3},{3,4},{4,5},{5,6},{6,7},{8,9},{9,10},{10,11},{11... | collective-permute-start | bytes 3145736 | tf_op jit(solution)/shard_map/ppermute | solution.py:217
  23.5 45.1 %collective-permute-start.1 = (bf16[4,131072]{1,0:T(4,128)(2,1)}, bf16[4,131072]{1,0:T(4,128)(2,1)S(1)}, u32[]{:S(2)}, u32[]{:S(2)}) collective-permute-start(bf16[4,131072]{1,0:T(4,128)(2,1)} %get-tuple-element.10), channel_id=1, source_target_pairs={{1,0},{2,1},{3,2},{4,3},{5,4},{6,5},{7,6},{9,8},{10,9},{11,10},{12... | collective-permute-start | bytes 3145736 | tf_op jit(solution)/shard_map/ppermute | solution.py:217
  24.8 37.7 %collective-permute-start.2 = (bf16[2,131072]{1,0:T(2,128)(2,1)}, bf16[2,131072]{1,0:T(2,128)(2,1)S(1)}, u32[]{:S(2)}, u32[]{:S(2)}) collective-permute-start(bf16[2,131072]{1,0:T(2,128)(2,1)} %get-tuple-element.11), channel_id=1, source_target_pairs={{0,8},{8,16},{16,24},{1,9},{9,17},{17,25},{2,10},{10,18},{18,26},{... | collective-permute-start | bytes 1572872 | tf_op jit(solution)/shard_map/ppermute | solution.py:217
  26.3 36.2 %collective-permute-start.3 = (bf16[2,131072]{1,0:T(2,128)(2,1)}, bf16[2,131072]{1,0:T(2,128)(2,1)S(1)}, u32[]{:S(2)}, u32[]{:S(2)}) collective-permute-start(bf16[2,131072]{1,0:T(2,128)(2,1)} %get-tuple-element.12), channel_id=1, source_target_pairs={{8,0},{16,8},{24,16},{9,1},{17,9},{25,17},{10,2},{18,10},{26,18},{... | collective-permute-start | bytes 1572872 | tf_op jit(solution)/shard_map/ppermute | solution.py:217
  62.5 6.2 %copy-start.2 = (bf16[2,131072]{1,0:T(2,128)(2,1)}, bf16[2,131072]{1,0:T(2,128)(2,1)S(1)}, u32[]{:S(2)}) copy-start(bf16[2,131072]{1,0:T(2,128)(2,1)S(1)} %collective-permute-done.2.left_ref) | copy-start | bytes 1572868
  62.5 6.2 %copy-start.3 = (bf16[2,131072]{1,0:T(2,128)(2,1)}, bf16[2,131072]{1,0:T(2,128)(2,1)S(1)}, u32[]{:S(2)}) copy-start(bf16[2,131072]{1,0:T(2,128)(2,1)S(1)} %collective-permute-done.3.right_ref) | copy-start | bytes 1572868
  68.6 1.0 copy-start
  69.7 1.0 copy-start.1

commit v2 on v1

--- a/solution.py
+++ b/solution.py
@@ -7,7 +7,8 @@
 from jax.sharding import PartitionSpec as P
 
 ITERS = 20
-WIDTH = 4096
+WIDTH = 16384
+EDGE_WIDTH = 16384
 SUBS = 4
 PER_DOT = 4
 
@@ -16,8 +17,7 @@
 mismatch_scale = 8.0
 
 
-def chunk_width(length):
-    width = WIDTH
+def chunk_width(length, width):
     while length % width:
         width //= 2
     return width
@@ -109,7 +109,7 @@
 
 def edges(weights):
     rows, columns, sides, length = weights.shape
-    width = chunk_width(length)
+    width = chunk_width(length, EDGE_WIDTH)
     row_shape = jax.ShapeDtypeStruct((columns, length), weights.dtype)
     column_shape = jax.ShapeDtypeStruct((rows, length), weights.dtype)
     row_spec = pl.BlockSpec((columns, width), lambda i: (0, i))
@@ -183,7 +183,7 @@
 
 def strip_sums(kernel, strips, pixels, weights, halos, name):
     rows, columns, sides, length = pixels.shape
-    width = chunk_width(length)
+    width = chunk_width(length, WIDTH)
     dots = group(strips)
     block = (rows, columns, sides, width)
     halo_specs = [pl.BlockSpec((h.shape[0], width), lambda i: (0, i)) for h in halos]

time: 125 us -> 99.9 us (0.80); the launches traced: 123 us -> 99.6 us
  Pallas kernels: 105 us -> 72.8 us
  waiting for transfers between devices: 6.15 us -> 14.5 us
    pallas_call x2, Pallas kernels: 66.3 us -> 45.7 us  [strip_sums(): pl.pallas_call(functools.partial(kernel, dots), grid=(length // width,),...]
    pallas_call x1, Pallas kernels: 18.6 us -> 7.51 us  [edges(): pl.pallas_call(edges_kernel, grid=(length // width,), in_specs=[pl.BlockS...]
    ppermute x4, waiting for transfers between devices: 6.15 us -> 14.5 us  [shift(): return lax.ppermute(array, axis, pairs)]
  transfers between devices with their start and end apart: 4 -> 4, of which waited for: 1 -> 1; matrix products, arithmetic and copies ran while one was open for 0% -> 0% of each run, Pallas kernels for 28% -> 27%
where the time goes in v2:
time: 99.9 us; the launch traced here: 99.6 us
  Pallas kernels  72.8 us (73%)
  waiting for transfers between devices  14.5 us (15%)
  starting transfers between devices  9 us (9%)
  local copies, waits for them, and re-layouts  3.22 us (3%)
    pallas_call x2, Pallas kernels, strip_sums(): pl.pallas_call(functools.partial(kernel, dots), grid=(length // width,),...  45.7 us
    pallas_call x1, Pallas kernels, settle(): pl.pallas_call(functools.partial(settle_kernel, inner, outer, shape), in_...  19.6 us
    ppermute x4, waiting for transfers between devices, shift(): return lax.ppermute(array, axis, pairs)  14.5 us
    ppermute x4, starting transfers between devices, shift(): return lax.ppermute(array, axis, pairs)  9 us
    pallas_call x1, Pallas kernels, edges(): pl.pallas_call(edges_kernel, grid=(length // width,), in_specs=[pl.BlockS...  7.51 us
    unnamed x9, local copies, waits for them, and re-layouts  3.22 us
  transfers between devices with their start and end apart: 4, of which 1 were waited for; matrix products, arithmetic and copies ran while one was open for 0% of the time, Pallas kernels for 27%

profile of v2, /device:TPU:0, one launch (start us, length us, event | category | flops | bytes accessed | tf_op | source)
XLA Modules:
  0.0 99.6 jit_solution(15253235956025314075)
XLA Ops:
  0.0 7.5 %edges.1 = (bf16[4,131072]{1,0:T(4,128)(2,1)}, bf16[4,131072]{1,0:T(4,128)(2,1)}, bf16[2,131072]{1,0:T(2,128)(2,1)}, bf16[2,131072]{1,0:T(2,128)(2,1)}) custom-call(bf16[2,4,4,131072]{3,2,1,0:T(4,128)(2,1)} %w_ref.5), custom_call_target="tpu_custom_call" | custom-call | tf_op jit(solution)/shard_map/edges/pallas_call | solution.py:117
  7.5 4.9 %collective-permute-start = (bf16[4,131072]{1,0:T(4,128)(2,1)}, bf16[4,131072]{1,0:T(4,128)(2,1)S(1)}, u32[]{:S(2)}, u32[]{:S(2)}) collective-permute-start(bf16[4,131072]{1,0:T(4,128)(2,1)} %get-tuple-element.9), channel_id=1, source_target_pairs={{0,1},{1,2},{2,3},{3,4},{4,5},{5,6},{6,7},{8,9},{9,10},{10,11},{11... | collective-permute-start | bytes 3145736 | tf_op jit(solution)/shard_map/ppermute | solution.py:217
  12.4 1.3 %collective-permute-start.1 = (bf16[4,131072]{1,0:T(4,128)(2,1)}, bf16[4,131072]{1,0:T(4,128)(2,1)S(1)}, u32[]{:S(2)}, u32[]{:S(2)}) collective-permute-start(bf16[4,131072]{1,0:T(4,128)(2,1)} %get-tuple-element.10), channel_id=1, source_target_pairs={{1,0},{2,1},{3,2},{4,3},{5,4},{6,5},{7,6},{9,8},{10,9},{11,10},{12... | collective-permute-start | bytes 3145736 | tf_op jit(solution)/shard_map/ppermute | solution.py:217
  13.7 1.5 %collective-permute-start.2 = (bf16[2,131072]{1,0:T(2,128)(2,1)}, bf16[2,131072]{1,0:T(2,128)(2,1)S(1)}, u32[]{:S(2)}, u32[]{:S(2)}) collective-permute-start(bf16[2,131072]{1,0:T(2,128)(2,1)} %get-tuple-element.11), channel_id=1, source_target_pairs={{0,8},{8,16},{16,24},{1,9},{9,17},{17,25},{2,10},{10,18},{18,26},{... | collective-permute-start | bytes 1572872 | tf_op jit(solution)/shard_map/ppermute | solution.py:217
  15.2 1.3 %collective-permute-start.3 = (bf16[2,131072]{1,0:T(2,128)(2,1)}, bf16[2,131072]{1,0:T(2,128)(2,1)S(1)}, u32[]{:S(2)}, u32[]{:S(2)}) collective-permute-start(bf16[2,131072]{1,0:T(2,128)(2,1)} %get-tuple-element.12), channel_id=1, source_target_pairs={{8,0},{16,8},{24,16},{9,1},{17,9},{25,17},{10,2},{18,10},{26,18},{... | collective-permute-start | bytes 1572872 | tf_op jit(solution)/shard_map/ppermute | solution.py:217
  16.5 26.5 %inner.1.inner_ref = f32[20,16,16]{2,1,0:T(8,128)} custom-call(s32[2,4,4,131072]{3,2,1,0:T(4,128)} %p_ref.3, bf16[2,4,4,131072]{3,2,1,0:T(4,128)(2,1)} %w_ref.5), custom_call_target="tpu_custom_call" | custom-call | flops 21474836480 | bytes 25165824 | tf_op jit(solution)/shard_map/inner/pallas_call | solution.py:194
  43.1 0.0 collective-permute-done.2.left_ref
  43.1 0.0 copy-start.2
  43.1 0.0 collective-permute-done.3.right_ref
  43.1 0.0 copy-start.3
  43.1 14.5 %collective-permute-done.up_ref = bf16[4,131072]{1,0:T(4,128)(2,1)S(1)} collective-permute-done((bf16[4,131072]{1,0:T(4,128)(2,1)}, bf16[4,131072]{1,0:T(4,128)(2,1)S(1)}, u32[]{:S(2)}, u32[]{:S(2)}) %collective-permute-start) | collective-permute-done | bytes 1048608 | tf_op jit(solution)/shard_map/ppermute | solution.py:217
  57.6 0.0 copy-start
  57.6 0.0 collective-permute-done.1.down_ref
  57.6 0.0 copy-done.2
  57.6 0.0 copy-done.3
  57.6 1.0 %copy-done = bf16[4,131072]{1,0:T(4,128)(2,1)} copy-done((bf16[4,131072]{1,0:T(4,128)(2,1)}, bf16[4,131072]{1,0:T(4,128)(2,1)S(1)}, u32[]{:S(2)}) %copy-start) | copy-done | bytes 1048600
  58.6 0.0 copy-start.1
  58.6 1.0 copy-done.1
  59.6 19.1 %outer.1.outer_ref = f32[12,16,16]{2,1,0:T(8,128)} custom-call(s32[2,4,4,131072]{3,2,1,0:T(4,128)} %p_ref.3, bf16[2,4,4,131072]{3,2,1,0:T(4,128)(2,1)} %w_ref.5, bf16[4,131072]{1,0:T(4,128)(2,1)} %copy-done, bf16[4,131072]{1,0:T(4,128)(2,1)} %copy-done.1, bf16[2,131072]{1,0:T(2,128)(2,1)} %copy-done.2, bf16[2,131072]{1,0:T(2,128)(2,1)} %copy-done.3), custom_call_target="tpu_custom_call" | custom-call | flops 12884901888 | bytes 25165824 | tf_op jit(solution)/shard_map/outer/pallas_call | solution.py:194
  78.7 19.6 %settle.1 = f32[2,4]{1,0:T(2,128)} custom-call(f32[20,16,16]{2,1,0:T(8,128)} %inner.1.inner_ref, f32[12,16,16]{2,1,0:T(8,128)} %outer.1.outer_ref, s32[2,16,16]{2,1,0:T(8,128)} %adjacency_ref.1), custom_call_target="tpu_custom_call" | custom-call | tf_op jit(solution)/shard_map/settle/pallas_call | solution.py:419
  98.3 1.2 %copy.5 = f32[2,4]{1,0:T(2,128)} copy(f32[2,4]{1,0:T(2,128)} %settle.1) | data formatting | bytes 64
Async XLA Ops:
  7.5 50.1 %collective-permute-start = (bf16[4,131072]{1,0:T(4,128)(2,1)}, bf16[4,131072]{1,0:T(4,128)(2,1)S(1)}, u32[]{:S(2)}, u32[]{:S(2)}) collective-permute-start(bf16[4,131072]{1,0:T(4,128)(2,1)} %get-tuple-element.9), channel_id=1, source_target_pairs={{0,1},{1,2},{2,3},{3,4},{4,5},{5,6},{6,7},{8,9},{9,10},{10,11},{11... | collective-permute-start | bytes 3145736 | tf_op jit(solution)/shard_map/ppermute | solution.py:217
  12.4 45.1 %collective-permute-start.1 = (bf16[4,131072]{1,0:T(4,128)(2,1)}, bf16[4,131072]{1,0:T(4,128)(2,1)S(1)}, u32[]{:S(2)}, u32[]{:S(2)}) collective-permute-start(bf16[4,131072]{1,0:T(4,128)(2,1)} %get-tuple-element.10), channel_id=1, source_target_pairs={{1,0},{2,1},{3,2},{4,3},{5,4},{6,5},{7,6},{9,8},{10,9},{11,10},{12... | collective-permute-start | bytes 3145736 | tf_op jit(solution)/shard_map/ppermute | solution.py:217
  13.7 29.3 %collective-permute-start.2 = (bf16[2,131072]{1,0:T(2,128)(2,1)}, bf16[2,131072]{1,0:T(2,128)(2,1)S(1)}, u32[]{:S(2)}, u32[]{:S(2)}) collective-permute-start(bf16[2,131072]{1,0:T(2,128)(2,1)} %get-tuple-element.11), channel_id=1, source_target_pairs={{0,8},{8,16},{16,24},{1,9},{9,17},{17,25},{2,10},{10,18},{18,26},{... | collective-permute-start | bytes 1572872 | tf_op jit(solution)/shard_map/ppermute | solution.py:217
  15.2 27.8 %collective-permute-start.3 = (bf16[2,131072]{1,0:T(2,128)(2,1)}, bf16[2,131072]{1,0:T(2,128)(2,1)S(1)}, u32[]{:S(2)}, u32[]{:S(2)}) collective-permute-start(bf16[2,131072]{1,0:T(2,128)(2,1)} %get-tuple-element.12), channel_id=1, source_target_pairs={{8,0},{16,8},{24,16},{9,1},{17,9},{25,17},{10,2},{18,10},{26,18},{... | collective-permute-start | bytes 1572872 | tf_op jit(solution)/shard_map/ppermute | solution.py:217
  43.1 14.5 %copy-start.2 = (bf16[2,131072]{1,0:T(2,128)(2,1)}, bf16[2,131072]{1,0:T(2,128)(2,1)S(1)}, u32[]{:S(2)}) copy-start(bf16[2,131072]{1,0:T(2,128)(2,1)S(1)} %collective-permute-done.2.left_ref) | copy-start | bytes 1572868
  43.1 14.5 %copy-start.3 = (bf16[2,131072]{1,0:T(2,128)(2,1)}, bf16[2,131072]{1,0:T(2,128)(2,1)S(1)}, u32[]{:S(2)}) copy-start(bf16[2,131072]{1,0:T(2,128)(2,1)S(1)} %collective-permute-done.3.right_ref) | copy-start | bytes 1572868
  57.6 1.0 %copy-start = (bf16[4,131072]{1,0:T(4,128)(2,1)}, bf16[4,131072]{1,0:T(4,128)(2,1)S(1)}, u32[]{:S(2)}) copy-start(bf16[4,131072]{1,0:T(4,128)(2,1)S(1)} %collective-permute-done.up_ref) | copy-start | bytes 3145732
  58.6 1.0 copy-start.1
